TPU v7x, 128 devices: a whole 4x4x4 slice. The times are simulated.
128 devices in a mesh: tenant: 32 (over z, x, y_lo), tp: 4 (over y_hi, core).
Axes of the slice: x: 4, y: 4 (y_hi: 2, y_lo: 2; y = y_hi * 2 + y_lo), z: 4, core: 2. Of those that a mesh axis runs over, the one named last changes fastest.
Arguments:
- src_tokens: bfloat16 [1536, 64, 1024], P('tenant'), may hold values from -64 to 64
- pair_tenant: int32 [1536], P('tenant'), may hold values from 0 to 31, as said below
- pair_length: int32 [1536], P('tenant'), may hold values from 1 to 64
- norm_gain: float32 [32, 1024], P('tenant'), may hold values from 0.1 to 1.9
- w_query: bfloat16 [32, 1024, 4096], P('tenant', None, 'tp'), may hold values from -1 to 1
- w_key: bfloat16 [32, 1024, 4096], P('tenant', None, 'tp'), may hold values from -1 to 1
- w_value: bfloat16 [32, 1024, 4096], P('tenant', None, 'tp'), may hold values from -0.1875 to 0.1875
- w_out: bfloat16 [32, 4096, 1024], P('tenant', 'tp'), may hold values from -0.09375 to 0.09375
- rel_bias: float32 [32, 32, 32], P('tenant', None, 'tp'), may hold values from -6 to 6
Outputs:
- layer_out: bfloat16 [65536, 1024], P(('tenant', 'tp'))
Inputs may be any that keep to these rules, and one draw needn't show every extreme that they name: `pair_tenant`: the pairs of one retriever shard bound for one tenant have pair_length summing to at most 64; in every draw some tenant receives exactly 64 tokens from every shard.
All inputs are finite; a program needn't handle non-finite values.
Results may differ from a plain program's by a relative error of at most 0.0065.
Values may be sent and summed in bfloat16 or wider, within the bound.
A program may use at most 128 MiB of HBM per device.

v0:
```python
import math

import jax
import jax.numpy as jnp
import numpy as np
from jax import lax
from jax.sharding import PartitionSpec as P


def in_blocks(value, dim, length):
    before, after = (value.shape[:dim], value.shape[dim + 1 :])
    return jnp.moveaxis(value.reshape(*before, length, -1, *after), dim, 0)


def summed_on_arrival(value, axis, dim):
    length = lax.axis_size(axis)
    pieces = lax.all_to_all(in_blocks(value, dim, length), axis, 0, 0, tiled=True)
    return jnp.sum(pieces.astype(jnp.float32), axis=0)


def bucket_grid(extent, buckets):
    offsets = np.arange(extent)[None, :] - np.arange(extent)[:, None]
    half_count = buckets // 2
    upward = np.where(offsets > 0, half_count, 0)
    distance = np.abs(offsets)
    exact_limit = half_count // 2
    ratio = np.maximum(distance, 1) / exact_limit
    spread_bucket = exact_limit + np.floor(
        np.log(ratio) / math.log(128.0 / exact_limit) * (half_count - exact_limit)
    ).astype(np.int32)
    spread_bucket = np.minimum(spread_bucket, half_count - 1)
    return (upward + np.where(distance < exact_limit, distance, spread_bucket)).astype(np.int32)


def rms_normed(tenant_rows, gain_row):
    values = tenant_rows.astype(jnp.float32)
    mean_square = jnp.mean(values * values, axis=-1, keepdims=True)
    return (values * lax.rsqrt(mean_square + 1e-06) * gain_row).astype(jnp.bfloat16)


def pack_rows(tokens, tenant, length, first_id, tenants):
    shard_pairs, slot_rows, feature_count = tokens.shape
    pair_order = jnp.arange(shard_pairs, dtype=jnp.int32)
    earlier = (tenant[:, None] == tenant[None, :]) & (pair_order[None, :] < pair_order[:, None])
    offset = jnp.sum(jnp.where(earlier, length[None, :], 0), axis=1)
    position = jnp.arange(slot_rows, dtype=jnp.int32)
    target = (tenant * slot_rows + offset)[:, None] + position[None, :]
    target = jnp.where(position[None, :] < length[:, None], target, tenants * slot_rows)
    flat_target = target.reshape(-1)
    packed = (
        jnp.zeros((tenants * slot_rows, feature_count), tokens.dtype)
        .at[flat_target]
        .set(tokens.reshape(-1, feature_count), mode="drop")
    )
    pair_ids = jnp.broadcast_to((first_id + pair_order)[:, None], target.shape).reshape(-1)
    segment = (
        jnp.full((tenants * slot_rows,), -1, jnp.int32).at[flat_target].set(pair_ids, mode="drop")
    )
    return (packed.reshape(tenants, slot_rows, feature_count), segment.reshape(tenants, slot_rows))


def attend(normed, segment, query_weight, key_weight, value_weight, bias_table, slot_rows, tenants):
    row_total = normed.shape[0]
    local_heads = bias_table.shape[1]
    head_size = query_weight.shape[1] // local_heads
    query_rows = jnp.dot(normed, query_weight, preferred_element_type=jnp.float32).astype(
        jnp.bfloat16
    )
    key_rows = jnp.dot(normed, key_weight, preferred_element_type=jnp.float32).astype(jnp.bfloat16)
    value_rows = jnp.dot(normed, value_weight, preferred_element_type=jnp.float32).astype(
        jnp.bfloat16
    )
    block_rows = slot_rows * min(max(1, 128 // slot_rows), tenants)
    block_count = row_total // block_rows
    bucket_index = jnp.asarray(bucket_grid(block_rows, bias_table.shape[0]))
    bucket_match = (
        bucket_index[:, :, None] == jnp.arange(bias_table.shape[0], dtype=jnp.int32)[None, None, :]
    ).astype(jnp.float32)
    position_bias = jnp.einsum(
        "qkb,bh->hqk", bucket_match, bias_table, precision=lax.Precision.HIGHEST
    )
    query_blocks = query_rows.reshape(block_count, block_rows, local_heads, head_size)
    key_blocks = key_rows.reshape(block_count, block_rows, local_heads, head_size)
    value_blocks = value_rows.reshape(block_count, block_rows, local_heads, head_size)
    scores = jnp.einsum(
        "bqhd,bkhd->bhqk", query_blocks, key_blocks, preferred_element_type=jnp.float32
    )
    scores = scores + position_bias[None]
    segment_blocks = segment.reshape(block_count, block_rows)
    allowed = (segment_blocks[:, :, None] == segment_blocks[:, None, :]) & (
        segment_blocks[:, None, :] >= 0
    )
    scores = jnp.where(allowed[:, None], scores, -1000000000.0)
    maxima = jnp.max(scores, axis=-1, keepdims=True)
    weights = jnp.exp(scores - maxima)
    probabilities = (weights / jnp.sum(weights, axis=-1, keepdims=True)).astype(jnp.bfloat16)
    context = jnp.einsum(
        "bhqk,bkhd->bqhd", probabilities, value_blocks, preferred_element_type=jnp.float32
    )
    return context.astype(jnp.bfloat16).reshape(row_total, local_heads * head_size)


def per_device(
    src_tokens, pair_tenant, pair_length, norm_gain, w_query, w_key, w_value, w_out, rel_bias
):
    tenants = lax.axis_size("tenant")
    shard_pairs, slot_rows, feature_count = src_tokens.shape
    first_id = lax.axis_index("tenant") * shard_pairs
    column_share = feature_count // lax.axis_size("tp")
    columns = lax.dynamic_slice_in_dim(
        src_tokens, lax.axis_index("tp") * column_share, column_share, 2
    )
    packed, segment = pack_rows(columns, pair_tenant, pair_length, first_id, tenants)
    arrived, arrived_segment = (
        lax.all_to_all(packed, "tenant", split_axis=0, concat_axis=0, tiled=True),
        lax.all_to_all(segment, "tenant", split_axis=0, concat_axis=0, tiled=True),
    )
    arrived = lax.all_gather(
        arrived.reshape(tenants * slot_rows, column_share), "tp", axis=1, tiled=True
    )
    arrived_segment = arrived_segment.reshape(-1)
    normed = rms_normed(arrived, norm_gain[0])
    context = attend(
        normed, arrived_segment, w_query[0], w_key[0], w_value[0], rel_bias[0], slot_rows, tenants
    )
    out_weight = w_out[0]
    row_total = arrived.shape[0]
    own_rows = row_total // lax.axis_size("tp")
    head_total = summed_on_arrival(
        jnp.dot(context, out_weight, preferred_element_type=jnp.float32).astype(jnp.bfloat16),
        "tp",
        0,
    )
    first_row = lax.axis_index("tp") * own_rows
    residual = lax.dynamic_slice_in_dim(arrived, first_row, own_rows, 0).astype(jnp.float32)
    occupied = lax.dynamic_slice_in_dim(arrived_segment, first_row, own_rows, 0) >= 0
    return jnp.where(occupied[:, None], residual + head_total, 0.0).astype(jnp.bfloat16)


def solution(mesh):
    in_specs = (
        P("tenant", None, None),
        P("tenant"),
        P("tenant"),
        P("tenant", None),
        P("tenant", None, "tp"),
        P("tenant", None, "tp"),
        P("tenant", None, "tp"),
        P("tenant", "tp", None),
        P("tenant", None, "tp"),
    )
    out_specs = P(("tenant", "tp"), None)
    return jax.shard_map(
        per_device, mesh=mesh, in_specs=in_specs, out_specs=out_specs, check_vma=False
    )
```

profile of v0, /device:TPU:34, one launch (start us, length us, event | category | flops | bytes accessed | tf_op | source)
XLA Modules:
  0.0 212.2 jit_solution(8039649190054375029)
XLA Ops:
  6.6 1.0 select_reduce_fusion
  7.6 0.7 multiply_add_fusion
  8.2 0.7 add_select_fusion.4
  9.1 2.7 %constant_dynamic-slice_fusion = bf16[48,64,256]{2,1,0:T(8,128)(2,1)} fusion(bf16[48,64,1024]{2,1,0:T(8,128)(2,1)} %param.10, s32[]{:T(128)S(6)} %select_n.50), kind=kLoop, calls=%fused_computation.55 | loop fusion | bytes 3145732 | tf_op jit(solution)/shard_map/dynamic_slice | solution.py:110
  11.8 14.2 %scatter_custom_fusion.1 = bf16[2048,256]{1,0:T(8,128)(2,1)S(1)} fusion(s32[3072]{0:T(1024)S(1)} %bitcast.57, bf16[3072,256]{1,0:T(8,128)(2,1)} %bitcast.55, bf16[]{:T(256)} %constant.10.clone.1), kind=kCustom, calls=%fused_computation.40 | custom fusion | bytes 1049088 | tf_op jit(solution)/shard_map/scatter | solution.py:53
  26.0 23.4 %all_to_all.19 = bf16[32,64,256]{2,1,0:T(8,128)(2,1)} all-to-all(bf16[32,64,256]{2,1,0:T(8,128)(2,1)S(1)} %bitcast.54), channel_id=1, replica_groups=mesh['tenant'=32,'tp'=4] {'tenant'}, dimensions={0} | all-to-all | bytes 2097152 | tf_op jit(solution)/shard_map/all_to_all | solution.py:115
  49.6 11.8 %scatter_custom_fusion = s32[2048]{0:T(1024)S(1)} fusion(s32[3072]{0:T(1024)S(1)} %bitcast.58, s32[3072]{0:T(1024)S(1)} %reshape.140, s32[]{:T(128)} %constant.18.clone.1), kind=kCustom, calls=%fused_computation.51 | custom fusion | bytes 8196 | tf_op jit(solution)/shard_map/scatter | solution.py:57
  61.4 0.7 all_to_all.12
  62.1 7.2 %all-to-all-start = ((s32[32,1,64]{2,1,0:T(1,128)}), s32[32,1,64]{2,1,0:T(1,128)S(1)}, u32[]{:S(2)}, u32[]{:S(2)}) async-start(s32[32,1,64]{2,1,0:T(1,128)} %all_to_all.12), calls=%async_computation | async-start | bytes 32768 | tf_op jit(solution)/shard_map/all_to_all | solution.py:116
  69.3 0.7 fusion.27
  70.3 5.2 %all-to-all-done = s32[32,1,64]{2,1,0:T(1,128)S(1)} async-done(((s32[32,1,64]{2,1,0:T(1,128)}), s32[32,1,64]{2,1,0:T(1,128)S(1)}, u32[]{:S(2)}, u32[]{:S(2)}) %all-to-all-start) | async-done | bytes 8224 | tf_op jit(solution)/shard_map/all_to_all | solution.py:116
  75.5 1.3 compare_and_fusion
  76.8 12.8 %all-gather.2.cloned.1.call-done = bf16[2048,1024]{1,0:T(8,128)(2,1)} async-done(((bf16[2048,256]{1,0:T(8,128)(2,1)}), bf16[2048,1024]{1,0:T(8,128)(2,1)}) %all-gather.2.cloned.1.call-update) | async-done | bytes 4194320 | tf_op jit(solution)/shard_map/all_gather | solution.py:118
  89.6 3.2 %fusion.1 = f32[2048]{0:T(1024)S(1)} fusion(bf16[2048,1024]{1,0:T(8,128)(2,1)} %all-gather.2.cloned.1.call-done), kind=kLoop, calls=%fused_computation.5 | loop fusion | flops 6289408 | bytes 4202496 | tf_op jit(solution)/shard_map/reduce_sum | solution.py:37
  93.1 4.8 %convert_bitcast_fusion.2 = bf16[256,8,8,128]{3,1,2,0:T(8,128)(2,1)S(1)} fusion(bf16[1,1024,1024]{2,1,0:T(8,128)(2,1)S(1)} %copy-done, bf16[2048,1024]{1,0:T(8,128)(2,1)S(1)} %copy-done.2, f32[1024]{0:T(1024)S(1)} %bitcast.59, f32[2048]{0:T(1024)S(1)} %add_rsqrt_fusion), kind=kOutput, calls=%fused_computation.26 | convolution fusion | flops 4305453056 | bytes 10498048 | tf_op jit(solution)/shard_map/dot_general | solution.py:66
  97.9 1.1 copy.36
  99.1 0.4 copy-done.6
  99.5 4.8 %convert_bitcast_fusion.1 = bf16[256,8,8,128]{3,1,2,0:T(8,128)(2,1)S(1)} fusion(bf16[1,1024,1024]{2,1,0:T(8,128)(2,1)S(1)} %copy-done.6, bf16[2048,1024]{1,0:T(8,128)(2,1)S(1)} %copy-done.2, f32[1024]{0:T(1024)S(1)} %bitcast.60, f32[2048]{0:T(1024)S(1)} %add_rsqrt_fusion), kind=kOutput, calls=%fused_computation.25 | convolution fusion | flops 4305453056 | bytes 10498048 | tf_op jit(solution)/shard_map/dot_general | solution.py:69
  104.4 1.1 copy.37
  106.0 5.1 %convert_bitcast_fusion.3 = bf16[256,8,8,128]{3,1,2,0:T(8,128)(2,1)S(1)} fusion(bf16[1,1024,1024]{2,1,0:T(8,128)(2,1)S(1)} %copy-done.7, bf16[2048,1024]{1,0:T(8,128)(2,1)S(1)} %copy-done.2, f32[1024]{0:T(1024)S(1)} %bitcast.61, f32[2048]{0:T(1024)S(1)} %add_rsqrt_fusion), kind=kOutput, calls=%fused_computation.27 | convolution fusion | flops 4305453056 | bytes 10498048 | tf_op jit(solution)/shard_map/dot_general | solution.py:70
  111.0 3.0 %copy.35 = bf16[256,8,8,128]{3,2,1,0:T(8,128)(2,1)} copy(bf16[256,8,8,128]{3,1,2,0:T(8,128)(2,1)S(1)} %convert_bitcast_fusion.3) | data formatting | bytes 8388608
  114.1 3.0 %fusion.10 = f32[16,8,128,128]{2,3,1,0:T(8,128)S(1)} fusion(bf16[16,128,8,128]{3,2,1,0:T(8,128)(2,1)S(1)} %bitcast.49, bf16[16,128,8,128]{3,2,1,0:T(8,128)(2,1)S(1)} %bitcast.48), kind=kOutput, calls=%fused_computation.18 | convolution fusion | flops 536870912 | bytes 16777216 | tf_op jit(solution)/shard_map/bqhd,bkhd->bhqk/dot_general | solution.py:85
  117.1 4.3 %fusion.39 = (f32[16,8,128]{2,1,0:T(8,128)S(1)}, f32[16,8,128,128]{2,3,1,0:T(8,128)}) fusion(f32[16,8,128,128]{2,3,1,0:T(8,128)S(1)} %fusion.10, f32[8,128,128]{1,2,0:T(8,128)S(1)} %copy.30, pred[16,128,128]{1,2,0:T(8,128)(4,1)S(1)} %copy-done.3), kind=kOutput, calls=%fused_computation.58 | output fusion | flops 12583039 | bytes 17629184 | tf_op jit(solution)/shard_map/sub | solution.py:95
  121.4 8.2 %convert_bitcast_fusion = bf16[16,128,8,128]{1,3,2,0:T(8,128)(2,1)} fusion(f32[16,8,128,128]{2,3,1,0:T(8,128)} %get-tuple-element.6, f32[16,8,128]{2,1,0:T(8,128)S(1)} %get-tuple-element.5, bf16[16,128,8,128]{3,2,1,0:T(8,128)(2,1)} %bitcast.51), kind=kOutput, calls=%fused_computation.21 | convolution fusion | flops 543162368 | bytes 16842752 | tf_op jit(solution)/shard_map/bhqk,bkhd->bqhd/dot_general | solution.py:97
  129.6 6.9 %copy.33 = bf16[16,128,8,128]{3,2,1,0:T(8,128)(2,1)} copy(bf16[16,128,8,128]{1,3,2,0:T(8,128)(2,1)} %convert_bitcast_fusion) | data formatting | bytes 8388608 | tf_op jit(solution)/shard_map/convert_element_type | solution.py:100
  136.5 8.3 %fusion.17 = bf16[2048,1024]{1,0:T(8,128)(2,1)} fusion(bf16[256,8,8,128]{3,2,1,0:T(8,128)(2,1)} %bitcast.52, bf16[1,1024,1024]{2,1,0:T(8,128)(2,1)S(1)} %copy-done.8), kind=kOutput, calls=%fused_computation.29 | convolution fusion | flops 4297064448 | bytes 10485760 | tf_op jit(solution)/shard_map/dot_general | solution.py:130
  144.9 4.9 %all-to-all-start.2 = ((bf16[4,512,1024]{2,1,0:T(8,128)(2,1)}), bf16[4,512,1024]{2,1,0:T(8,128)(2,1)}, u32[]{:S(2)}, u32[]{:S(2)}) async-start(bf16[4,512,1024]{2,1,0:T(8,128)(2,1)} %bitcast.50), calls=%async_computation.2 | async-start | bytes 8388608 | tf_op jit(solution)/shard_map/all_to_all | solution.py:17
  149.7 0.5 broadcast.81
  150.2 0.7 reduce.5
  151.1 48.3 %all-to-all-done.2 = bf16[4,512,1024]{2,1,0:T(8,128)(2,1)} async-done(((bf16[4,512,1024]{2,1,0:T(8,128)(2,1)}), bf16[4,512,1024]{2,1,0:T(8,128)(2,1)}, u32[]{:S(2)}, u32[]{:S(2)}) %all-to-all-start.2) | async-done | bytes 4194336 | tf_op jit(solution)/shard_map/all_to_all | solution.py:17
  199.4 3.4 %convert_reduce_fusion = f32[512,1024]{1,0:T(8,128)S(1)} fusion(bf16[4,512,1024]{2,1,0:T(8,128)(2,1)} %all-to-all-done.2), kind=kLoop, calls=%fused_computation.8 | loop fusion | flops 3670016 | bytes 6291456 | tf_op jit(solution)/shard_map/reduce_sum | solution.py:18
  202.8 2.5 %select_convert_fusion = bf16[512,1024]{1,0:T(8,128)(2,1)} fusion(f32[512,1024]{1,0:T(8,128)S(1)} %convert_reduce_fusion, bf16[2048,1024]{1,0:T(8,128)(2,1)} %all-gather.2.cloned.1.call-done, s32[]{:T(128)S(6)} %select_n.49, pred[512]{0:T(512)(128)(4,1)S(1)} %dynamic-slice_compare_fusion), kind=kLoop, calls=%fused_computation.34 | loop fusion | flops 2097152 | bytes 4194820 | tf_op jit(solution)/shard_map/convert_element_type | solution.py:137
  (32 shorter events, 1.4 us)
Async XLA Ops:
  6.5 86.3 %copy-start = (bf16[1,1024,1024]{2,1,0:T(8,128)(2,1)S(1)}, bf16[1,1024,1024]{2,1,0:T(8,128)(2,1)}, u32[]{:S(2)}) copy-start(bf16[1,1024,1024]{2,1,0:T(8,128)(2,1)} %param.14) | copy-start | bytes 6291460
  6.5 62.7 %copy-start.4 = (s32[128,128]{1,0:T(8,128)S(1)}, s32[128,128]{1,0:T(8,128)}, u32[]{:S(2)}) copy-start(s32[128,128]{1,0:T(8,128)} %constant.44.clone) | copy-start | bytes 196612
  6.5 62.7 %copy-start.5 = (f32[1,32,8]{1,2,0:T(8,128)S(1)}, f32[1,32,8]{1,2,0:T(8,128)}, u32[]{:S(2)}) copy-start(f32[1,32,8]{1,2,0:T(8,128)} %param.18) | copy-start | bytes 3076
  6.5 83.1 %all-gather.2.cloned.1.call-start = ((), (), s32[]{:S(2)}) async-start(), calls=%async_computation.3 | async-start | bytes 5242880 | tf_op jit(solution)/shard_map/all_gather | solution.py:118
  49.4 43.5 %copy-start.9 = (f32[1,1024]{1,0:T(1,128)S(1)}, f32[1,1024]{1,0:T(1,128)}, u32[]{:S(2)}) copy-start(f32[1,1024]{1,0:T(1,128)} %param.13) | copy-start | bytes 12292
  62.1 13.3 %all-to-all-start = ((s32[32,1,64]{2,1,0:T(1,128)}), s32[32,1,64]{2,1,0:T(1,128)S(1)}, u32[]{:S(2)}, u32[]{:S(2)}) async-start(s32[32,1,64]{2,1,0:T(1,128)} %all_to_all.12), calls=%async_computation | async-start | bytes 32768 | tf_op jit(solution)/shard_map/all_to_all | solution.py:116
  89.6 3.4 %copy-start.2 = (bf16[2048,1024]{1,0:T(8,128)(2,1)S(1)}, bf16[2048,1024]{1,0:T(8,128)(2,1)}, u32[]{:S(2)}) copy-start(bf16[2048,1024]{1,0:T(8,128)(2,1)} %all-gather.2.cloned.1.call-done) | copy-start | bytes 12582916
  97.9 1.6 copy-start.6
  104.4 1.6 copy-start.7
  114.1 3.0 %copy-start.3 = (pred[16,128,128]{1,2,0:T(8,128)(4,1)S(1)}, pred[16,128,128]{1,2,0:T(8,128)(4,1)}, u32[]{:S(2)}) copy-start(pred[16,128,128]{1,2,0:T(8,128)(4,1)} %compare_and_fusion) | copy-start | bytes 786436
  129.6 6.9 %copy-start.8 = (bf16[1,1024,1024]{2,1,0:T(8,128)(2,1)S(1)}, bf16[1,1024,1024]{2,1,0:T(8,128)(2,1)}, u32[]{:S(2)}) copy-start(bf16[1,1024,1024]{2,1,0:T(8,128)(2,1)} %param.17) | copy-start | bytes 6291460
  144.9 54.6 %all-to-all-start.2 = ((bf16[4,512,1024]{2,1,0:T(8,128)(2,1)}), bf16[4,512,1024]{2,1,0:T(8,128)(2,1)}, u32[]{:S(2)}, u32[]{:S(2)}) async-start(bf16[4,512,1024]{2,1,0:T(8,128)(2,1)} %bitcast.50), calls=%async_computation.2 | async-start | bytes 8388608 | tf_op jit(solution)/shard_map/all_to_all | solution.py:17
  151.0 54.4 %copy-start.1 = (bf16[1,1024,1024]{2,1,0:T(8,128)(2,1)S(1)}, bf16[1,1024,1024]{2,1,0:T(8,128)(2,1)}, u32[]{:S(2)}) copy-start(bf16[1,1024,1024]{2,1,0:T(8,128)(2,1)} %param.14) | copy-start | bytes 6291460
Sparse Core Ops, SparseCore 0:
  49.6 40.0 all-gather.1
where the time goes:
time: 214 us; the launch traced here: 212 us
  waiting for transfers between devices  66.3 us (31%)
  local copies, waits for them, and re-layouts  43.8 us (20%)
  matrix products  35.1 us (16%)
  blocking collectives  23.4 us (11%)
  other arithmetic  18 us (8%)
  between operations  13.6 us (6%)
  starting transfers between devices  12 us (6%)
    all_to_all x1, waiting for transfers between devices, summed_on_arrival(): lax.all_to_all(in_blocks(value, dim, length), axis, 0, 0, tiled=True)  48.3 us
    all_to_all x1, blocking collectives, per_device(): lax.all_to_all(packed, 'tenant', split_axis=0, concat_axis=0, tiled=True)  23.4 us
    scatter x1, local copies, waits for them, and re-layouts, pack_rows(): packed = jnp.zeros((tenants * slot_rows, feature_count), tokens.dtype).at...  14.2 us
    all_gather x1, waiting for transfers between devices, per_device(): lax.all_gather(arrived.reshape(tenants * slot_rows, column_share), 'tp',...  12.8 us
    scatter x1, local copies, waits for them, and re-layouts, pack_rows(): jnp.full((tenants * slot_rows,), -1, jnp.int32).at[flat_target]  11.8 us
    dot_general x1, matrix products, per_device(): jnp.dot(context, out_weight, preferred_element_type=jnp.float32)  8.33 us
    dot_general x1, matrix products, attend(): jnp.einsum('bhqk,bkhd->bqhd', probabilities, value_blocks, preferred_elem...  8.23 us
    all_to_all x1, starting transfers between devices, per_device(): lax.all_to_all(segment, 'tenant', split_axis=0, concat_axis=0, tiled=True)  7.18 us
  transfers between devices with their start and end apart: 3, of which 3 were waited for; matrix products, arithmetic and copies ran while one was open for 7% of the time, Pallas kernels for 0%

commit v1 on v0

v1 whole, which is shorter than its diff:
```python
import functools
import math

import jax
import jax.numpy as jnp
import numpy as np
from jax import lax
from jax.experimental import pallas as pl
from jax.experimental.pallas import tpu as pltpu
from jax.sharding import PartitionSpec as P

MESH = pl.DeviceIdType.MESH
CAP = 64
D = 1024
HALF = 512
SLOTS = 32
GROUPS = 8
HEADS = 8
DK = 128
NEG = -1e30
EPS = 1e-6


def bucket_grid(extent, buckets):
    offsets = np.arange(extent)[None, :] - np.arange(extent)[:, None]
    half_count = buckets // 2
    upward = np.where(offsets > 0, half_count, 0)
    distance = np.abs(offsets)
    exact_limit = half_count // 2
    ratio = np.maximum(distance, 1) / exact_limit
    spread_bucket = exact_limit + np.floor(
        np.log(ratio) / math.log(128.0 / exact_limit) * (half_count - exact_limit)
    ).astype(np.int32)
    spread_bucket = np.minimum(spread_bucket, half_count - 1)
    return (upward + np.where(distance < exact_limit, distance, spread_bucket)).astype(np.int32)


def position_bias(table):
    grid = bucket_grid(CAP, table.shape[0])
    grid = np.concatenate([grid, grid], axis=1)
    match = jnp.asarray(
        (grid[:, :, None] == np.arange(table.shape[0])[None, None, :]).astype(np.float32)
    )
    return jnp.einsum("qkb,bh->hqk", match, table, precision=lax.Precision.HIGHEST)


def pack_kernel(tenant_ref, length_ref, src_ref, packed_ref, meta_ref, tokens, stage, fill, sems):
    core = lax.rem(lax.axis_index("tp"), 2)
    pairs = src_ref.shape[0]
    step = pairs // 4
    copies = []
    for i in range(4):
        copies.append(
            pltpu.make_async_copy(
                src_ref.at[pl.ds(i * step, step), :, pl.ds(pl.multiple_of(core * HALF, HALF), HALF)],
                tokens.at[pl.ds(i * step, step)],
                sems.at[i],
            )
        )
        copies[-1].start()

    def clear(u, _):
        fill[u] = 0
        return 0

    lax.fori_loop(0, SLOTS, clear, 0)
    meta_ref[...] = jnp.zeros_like(meta_ref)
    lane = lax.broadcasted_iota(jnp.int32, (1, 128), 1)

    def place(i, _):
        u = tenant_ref[i]
        n = length_ref[i]
        start = fill[u]
        fill[u] = start + n
        code = start * 256 + start + n
        inside = ((lane % CAP) >= start) & ((lane % CAP) < start + n)
        meta_ref[u] = jnp.where(inside, code, meta_ref[u])
        for c in range(4):
            piece = tokens[i, :, c * 128 : c * 128 + 128].astype(jnp.float32)
            stage[u, c, pl.ds(start, CAP), :] = piece
        return 0

    for i in range(4):
        copies[i].wait()
        lax.fori_loop(i * step, (i + 1) * step, place, 0)
    row = lax.broadcasted_iota(jnp.int32, (CAP, 128), 0)

    def finish(u, _):
        for c in range(4):
            rows = jnp.where(row < fill[u], stage[u, c, 0:CAP, :], 0.0).astype(jnp.bfloat16)
            packed_ref[u, :, c * 128 : c * 128 + 128] = rows
        return 0

    lax.fori_loop(0, SLOTS, finish, 0)


def pack(tenant, length, tokens):
    pairs = tokens.shape[0]
    smem = pl.BlockSpec(memory_space=pltpu.SMEM)
    vmem = pl.BlockSpec(memory_space=pltpu.VMEM)
    return pl.pallas_call(
        pack_kernel,
        out_shape=(
            jax.ShapeDtypeStruct((SLOTS, CAP, HALF), jnp.bfloat16),
            jax.ShapeDtypeStruct((SLOTS, 1, 128), jnp.int32),
        ),
        in_specs=[smem, smem, pl.BlockSpec(memory_space=pl.ANY)],
        out_specs=(vmem, vmem),
        scratch_shapes=[
            pltpu.VMEM((pairs, CAP, HALF), jnp.bfloat16),
            pltpu.VMEM((SLOTS, 4, 2 * CAP, 128), jnp.float32),
            pltpu.SMEM((SLOTS,), jnp.int32),
            pltpu.SemaphoreType.DMA((4,)),
        ],
        compiler_params=pltpu.CompilerParams(vmem_limit_bytes=40 * 1024 * 1024),
        name="pack",
    )(tenant, length, tokens)


def here():
    t = lax.axis_index("tenant")
    p = lax.axis_index("tp")
    return t // 8, (t // 2) % 4, t % 2, p // 2, p % 2


def device(z, x, lo, hi, core):
    return ((z % 4) * 8 + (x % 4) * 2 + lo % 2, (hi % 2) * 2 + core % 2)


def shift_of(pos):
    g = pos // 4
    a = (pos // 2) % 2
    b = pos % 2
    dz = g % 2 + 2 * a
    dx = (g // 2 + b) % 4
    return dz, dx, b


def layer_kernel(
    packed_ref, meta_ref, gain_ref, bias_ref, wq_hbm, wk_hbm, wv_hbm, wo_hbm, out_ref,
    wq, wk, wv, wo, arr, codes, normed, query, key, value, context, part,
    keep, pair_out, pair_in, mate_out, mate_in, far_out, far_in, mine,
    wsem, tok_s, tok_r, meta_s, meta_r, fwd_s, fwd_r,
    pair_s, pair_r, mate_s, mate_r, far_s, far_r,
):
    z, x, lo, hi, core = here()
    tenant = lax.axis_index("tenant")
    partner = device(z, x, lo, hi, core + 1)

    def peer(pos):
        dz, dx, dl = shift_of(pos)
        return device(z + dz, x + dx, lo + dl, hi + dl * ((dz + dx) % 2), core)

    weights = [
        pltpu.make_async_copy(src.at[0], dst, wsem.at[i])
        for i, (src, dst) in enumerate(((wq_hbm, wq), (wk_hbm, wk), (wv_hbm, wv), (wo_hbm, wo)))
    ]
    for copy in weights:
        copy.start()

    barrier = pltpu.get_barrier_semaphore()

    def greet(pos, _):
        pl.semaphore_signal(barrier, inc=1, device_id=peer(pos), device_id_type=MESH)
        return 0

    lax.fori_loop(1, SLOTS, greet, 0)
    pl.semaphore_signal(barrier, inc=1, device_id=partner, device_id_type=MESH)
    for c in range(2):
        pl.semaphore_signal(
            barrier, inc=1, device_id=device(z, x, lo, hi + 1, c), device_id_type=MESH
        )
    pl.semaphore_wait(barrier, SLOTS + 2)

    def token_copy(pos):
        target = peer(pos)
        return pltpu.make_async_remote_copy(
            packed_ref.at[target[0]], arr.at[core, pos], tok_s.at[pos], tok_r.at[pos],
            device_id=target, device_id_type=MESH,
        )

    def meta_copy(pos):
        target = peer(pos)
        return pltpu.make_async_remote_copy(
            meta_ref.at[target[0]], codes.at[pos], meta_s.at[pos], meta_r.at[pos],
            device_id=target, device_id_type=MESH,
        )

    def forward_copy(pos):
        return pltpu.make_async_remote_copy(
            arr.at[core, pos], arr.at[core, pos], fwd_s.at[pos], fwd_r.at[pos],
            device_id=partner, device_id_type=MESH,
        )

    own_forward = pltpu.make_async_remote_copy(
        packed_ref.at[tenant], arr.at[core, 0], fwd_s.at[0], fwd_r.at[0],
        device_id=partner, device_id_type=MESH,
    )
    def wait_partner(pos):
        pltpu.make_async_remote_copy(
            arr.at[1 - core, pos], arr.at[1 - core, pos], fwd_s.at[pos], fwd_r.at[pos],
            device_id=partner, device_id_type=MESH,
        ).wait_recv()

    own_forward.start()

    def send(pos, _):
        meta_copy(pos).start()
        token_copy(pos).start()
        return 0

    lax.fori_loop(1, SLOTS, send, 0)
    arr[core, 0] = packed_ref[tenant]
    codes[0] = meta_ref[tenant]

    def receive(pos):
        token_copy(pos).wait_recv()
        meta_copy(pos).wait_recv()
        forward_copy(pos).start()

    for pos in range(1, 4):
        receive(pos)

    def planes(g):
        first = (z + 4 - g % 2) % 4
        other = (first + 2) % 4
        first_far = jnp.where(first // 2 != hi, 1, 0)
        far_pair = 1 - first_far
        far_plane = jnp.where(first_far == 1, first, other)
        near_plane = jnp.where(first_far == 1, other, first)
        return far_pair, far_plane, near_plane

    def pair_copy(g):
        return pltpu.make_async_remote_copy(
            pair_out.at[g], pair_in.at[g], pair_s.at[g], pair_r.at[g],
            device_id=partner, device_id_type=MESH,
        )

    def mate_copy(q):
        return pltpu.make_async_remote_copy(
            mate_out.at[q], mate_in.at[q], mate_s.at[q], mate_r.at[q],
            device_id=partner, device_id_type=MESH,
        )

    def far_copy(g):
        _, far_plane, _ = planes(g)
        return pltpu.make_async_remote_copy(
            far_out.at[g], far_in.at[core, g // 2], far_s.at[g], far_r.at[core, g // 2],
            device_id=device(z, x, lo, hi + 1, far_plane), device_id_type=MESH,
        )

    def finish_pair(g):
        pair_copy(g).wait_recv()
        total = keep[g % 2] + pair_in[g].astype(jnp.float32)
        far_out[g] = total.astype(jnp.bfloat16)
        far_copy(g).start()

    row = lax.broadcasted_iota(jnp.int32, (128, 128), 0)
    col = lax.broadcasted_iota(jnp.int32, (128, 128), 1)

    def group(g, _):
        base = g * 4
        for i in range(4):
            wait_partner(base + i)
        left = arr[0, pl.ds(base, 4)].reshape(256, HALF).astype(jnp.float32)
        right = arr[1, pl.ds(base, 4)].reshape(256, HALF).astype(jnp.float32)
        mean = (
            jnp.sum(left * left, axis=-1, keepdims=True)
            + jnp.sum(right * right, axis=-1, keepdims=True)
        ) / D
        scale = lax.rsqrt(mean + EPS)
        normed[:, 0:HALF] = (left * scale * gain_ref[:, 0:HALF]).astype(jnp.bfloat16)
        normed[:, HALF:D] = (right * scale * gain_ref[:, HALF:D]).astype(jnp.bfloat16)

        @pl.when(g == 0)
        def _():
            for copy in weights:
                copy.wait()

        rows = normed[...]
        query[...] = jnp.dot(rows, wq[...], preferred_element_type=jnp.float32).astype(jnp.bfloat16)
        key[...] = jnp.dot(rows, wk[...], preferred_element_type=jnp.float32).astype(jnp.bfloat16)
        value[...] = jnp.dot(rows, wv[...], preferred_element_type=jnp.float32).astype(jnp.bfloat16)

        @pl.when(g > 0)
        def _():
            finish_pair(g - 1)

        @pl.when(g < GROUPS - 1)
        def _():
            for i in range(4):
                receive(base + 4 + i)

        for block in range(2):
            code = jnp.where(col[0:1] < CAP, codes[base + 2 * block], codes[base + 2 * block + 1])
            shift = jnp.where(col[0:1] < CAP, 0, CAP)
            start = code // 256 + shift
            end = code % 256 + shift
            allowed = (row >= start) & (row < end)
            span = slice(block * 128, block * 128 + 128)
            for h in range(HEADS):
                lanes = slice(h * DK, h * DK + DK)
                s = lax.dot_general(
                    query[span, lanes], key[span, lanes], (((1,), (1,)), ((), ())),
                    preferred_element_type=jnp.float32,
                )
                b = bias_ref[h]
                s = jnp.where(allowed, s + jnp.concatenate([b, b], axis=0), NEG)
                top = jnp.max(s, axis=-1, keepdims=True)
                w = jnp.exp(s - top)
                total = jnp.sum(w, axis=-1, keepdims=True)
                inverse = jnp.where(top > 0.5 * NEG, 1.0 / total, 0.0)
                ctx = jnp.dot(
                    (w * inverse).astype(jnp.bfloat16), value[span, lanes],
                    preferred_element_type=jnp.float32,
                )
                context[span, lanes] = ctx.astype(jnp.bfloat16)

        part[...] = jnp.dot(context[...], wo[...], preferred_element_type=jnp.float32)
        far_pair, _, near_plane = planes(g)
        far_rows = pl.ds(pl.multiple_of(far_pair * 128, 128), 128)
        near_rows = pl.ds(pl.multiple_of((1 - far_pair) * 128, 128), 128)
        own_cols = pl.ds(pl.multiple_of(core * HALF, HALF), HALF)
        other_cols = pl.ds(pl.multiple_of((1 - core) * HALF, HALF), HALF)
        pair_out[g] = part[far_rows, other_cols].astype(jnp.bfloat16)
        pair_copy(g).start()
        keep[g % 2] = part[far_rows, own_cols]

        @pl.when(near_plane % 2 == core)
        def _():
            mine[g // 2] = part[near_rows, :]

        @pl.when(near_plane % 2 != core)
        def _():
            mate_out[g // 2] = part[near_rows, :].astype(jnp.bfloat16)
            mate_copy(g // 2).start()

        return 0

    lax.fori_loop(0, GROUPS, group, 0)
    finish_pair(GROUPS - 1)

    plane = hi * 2 + core
    parity = (z + plane) % 2

    def combine(q, _):
        g = 2 * q + parity
        far_pair, _, _ = planes(g)
        near_pair = 1 - far_pair
        mate_copy(q).wait_recv()
        for c in range(2):
            pltpu.make_async_remote_copy(
                far_in.at[c, q], far_in.at[c, q], far_s.at[q], far_r.at[c, q],
                device_id=partner, device_id_type=MESH,
            ).wait_recv()
        for b in range(2):
            pos = g * 4 + near_pair * 2 + b
            src_slot = ((x + 8 - q - b) % 4) * 2 + (lo + b) % 2
            span = slice(b * CAP, b * CAP + CAP)
            for c in range(2):
                cols = slice(c * HALF, c * HALF + HALF)
                total = (
                    mine[q, span, cols]
                    + mate_in[q, span, cols].astype(jnp.float32)
                    + far_in[c, q, span, :].astype(jnp.float32)
                    + arr[c, pos].astype(jnp.float32)
                )
                out_ref[src_slot, :, cols] = total.astype(jnp.bfloat16)
        return 0

    lax.fori_loop(0, 4, combine, 0)

    def drain(pos, _):
        token_copy(pos).wait_send()
        meta_copy(pos).wait_send()
        forward_copy(pos).wait_send()
        return 0

    own_forward.wait_send()
    lax.fori_loop(1, SLOTS, drain, 0)

    def drain_groups(g, _):
        pair_copy(g).wait_send()
        far_copy(g).wait_send()
        return 0

    lax.fori_loop(0, GROUPS, drain_groups, 0)

    def drain_mates(q, _):
        mate_copy(q).wait_send()
        return 0

    lax.fori_loop(0, 4, drain_mates, 0)


def layer(packed, meta, gain, bias, wq, wk, wv, wo):
    vmem = pl.BlockSpec(memory_space=pltpu.VMEM)
    anywhere = pl.BlockSpec(memory_space=pl.ANY)
    bf, f32 = jnp.bfloat16, jnp.float32
    dma = pltpu.SemaphoreType.DMA
    return pl.pallas_call(
        layer_kernel,
        out_shape=jax.ShapeDtypeStruct((8, CAP, D), bf),
        in_specs=[vmem] * 4 + [anywhere] * 4,
        out_specs=vmem,
        scratch_shapes=[pltpu.VMEM((D, D), bf)] * 4
        + [
            pltpu.VMEM((2, SLOTS, CAP, HALF), bf),
            pltpu.VMEM((SLOTS, 1, 128), jnp.int32),
        ]
        + [pltpu.VMEM((256, D), bf)] * 5
        + [
            pltpu.VMEM((256, D), f32),
            pltpu.VMEM((2, 128, HALF), f32),
            pltpu.VMEM((GROUPS, 128, HALF), bf),
            pltpu.VMEM((GROUPS, 128, HALF), bf),
            pltpu.VMEM((4, 128, D), bf),
            pltpu.VMEM((4, 128, D), bf),
            pltpu.VMEM((GROUPS, 128, HALF), bf),
            pltpu.VMEM((2, 4, 128, HALF), bf),
            pltpu.VMEM((4, 128, D), f32),
            dma((4,)), dma((SLOTS,)), dma((SLOTS,)), dma((SLOTS,)), dma((SLOTS,)),
            dma((SLOTS,)), dma((SLOTS,)),
            dma((GROUPS,)), dma((GROUPS,)), dma((4,)), dma((4,)), dma((GROUPS,)), dma((2, 4)),
        ],
        compiler_params=pltpu.CompilerParams(
            collective_id=0, has_side_effects=True, vmem_limit_bytes=56 * 1024 * 1024
        ),
        name="layer",
    )(packed, meta, gain, bias, wq, wk, wv, wo)


def per_device(
    src_tokens, pair_tenant, pair_length, norm_gain, w_query, w_key, w_value, w_out, rel_bias
):
    packed, meta = pack(pair_tenant, pair_length, src_tokens)
    bias = position_bias(rel_bias[0])
    out = layer(packed, meta, norm_gain, bias, w_query, w_key, w_value, w_out)
    return out.reshape(8 * CAP, D)


def solution(mesh):
    in_specs = (
        P("tenant", None, None),
        P("tenant"),
        P("tenant"),
        P("tenant", None),
        P("tenant", None, "tp"),
        P("tenant", None, "tp"),
        P("tenant", None, "tp"),
        P("tenant", "tp", None),
        P("tenant", None, "tp"),
    )
    out_specs = P(("tenant", "tp"), None)
    return jax.shard_map(
        per_device, mesh=mesh, in_specs=in_specs, out_specs=out_specs, check_vma=False
    )
```

time: 214 us -> 117 us (0.55)
  Pallas kernels: 0 us -> 105 us
  waiting for transfers between devices: 66.3 us -> 0 us
  local copies, waits for them, and re-layouts: 43.8 us -> 9.74 us
  matrix products: 35.1 us -> 1.88 us
  blocking collectives: 23.4 us -> 0 us
  other arithmetic: 18 us -> 0 us
  between operations: 13.6 us -> 0.04 us
  starting transfers between devices: 12 us -> 0 us
    pallas_call x0 -> x2, Pallas kernels: none -> 105 us  [the longest x1 102 us: layer(): pl.pallas_call(layer_kernel, out_shape=jax.ShapeDtypeStruct((8, CAP, D),...]
    all_to_all x2 -> x0, waiting for transfers between devices: 53.5 us -> none  [the longest x1 48.3 us: summed_on_arrival(): lax.all_to_all(in_blocks(value, dim, length), axis, 0, 0, tiled=True)]
    dot_general x7 -> x1, matrix products: 35.1 us -> 1.88 us  [position_bias(): jnp.einsum('qkb,bh->hqk', match, table, precision=lax.Precision.HIGHEST)]
    scatter x2 -> x0, local copies, waits for them, and re-layouts: 26 us -> none  [the longest x1 14.2 us: pack_rows(): packed = jnp.zeros((tenants * slot_rows, feature_count), tokens.dtype).at...]
    all_to_all x1 -> x0, blocking collectives: 23.4 us -> none  [per_device(): lax.all_to_all(packed, 'tenant', split_axis=0, concat_axis=0, tiled=True)]
    all_gather x1 -> x0, waiting for transfers between devices: 12.8 us -> none  [per_device(): lax.all_gather(arrived.reshape(tenants * slot_rows, column_share), 'tp',...]
    all_to_all x2 -> x0, starting transfers between devices: 12 us -> none  [the longest x1 7.18 us: per_device(): lax.all_to_all(segment, 'tenant', split_axis=0, concat_axis=0, tiled=True)]
    reduce_sum x3 -> x0, other arithmetic: 7.64 us -> none  [the longest x1 3.41 us: summed_on_arrival(): return jnp.sum(pieces.astype(jnp.float32), axis=0)]
  transfers between devices with their start and end apart: 3 -> 0, of which waited for: 3 -> 0; matrix products, arithmetic and copies ran while one was open for 7% -> 0% of each run, Pallas kernels for 0% -> 0%
where the time goes in v1:
time: 117 us; the launch traced here: 116 us
  Pallas kernels  105 us (90%)
  local copies, waits for them, and re-layouts  9.74 us (8%)
  matrix products  1.88 us (2%)
    pallas_call x1, Pallas kernels, layer(): pl.pallas_call(layer_kernel, out_shape=jax.ShapeDtypeStruct((8, CAP, D),...  102 us
    unnamed x13, local copies, waits for them, and re-layouts  8.99 us
    pallas_call x1, Pallas kernels, pack(): pl.pallas_call(pack_kernel, out_shape=(jax.ShapeDtypeStruct((SLOTS, CAP,...  2.63 us

profile of v1, /device:TPU:34, one launch (start us, length us, event | category | flops | bytes accessed | tf_op | source)
XLA Modules:
  0.0 116.4 jit_solution(5623294102542144501)
XLA Ops:
  0.0 0.0 copy-start
  0.0 0.7 copy-done
  0.7 1.9 %fusion = f32[64,128,8]{1,2,0:T(8,128)S(1)} fusion(f32[64,128,32]{1,2,0:T(8,128)} %constant.2.clone, f32[1,32,8]{1,2,0:T(8,128)S(1)} %copy-done), kind=kOutput, calls=%fused_computation.1 | convolution fusion | flops 25165824 | bytes 1311744 | tf_op jit(solution)/shard_map/qkb,bh->hqk/dot_general | solution.py:44
  2.6 0.8 copy.13
  3.3 0.0 copy-start.1
  3.3 2.8 %copy-done.1 = bf16[48,64,1024]{2,1,0:T(8,128)(2,1)S(1)} copy-done((bf16[48,64,1024]{2,1,0:T(8,128)(2,1)S(1)}, bf16[48,64,1024]{2,1,0:T(8,128)(2,1)}, u32[]{:S(2)}) %copy-start.1) | copy-done | bytes 6291480
  6.1 0.0 copy-start.4
  6.1 0.7 copy-done.4
  6.8 0.0 copy-start.5
  6.8 0.7 copy-done.5
  7.4 2.6 %pack.1 = (bf16[32,64,512]{2,1,0:T(8,128)(2,1)S(1)}, s32[32,1,128]{2,1,0:T(1,128)S(1)}) custom-call(s32[48]{0:T(128)S(1)} %copy-done.4, s32[48]{0:T(128)S(1)} %copy-done.5, bf16[48,64,1024]{2,1,0:T(8,128)(2,1)S(1)} %copy-done.1), custom_call_target="tpu_custom_call" | custom-call | tf_op jit(solution)/shard_map/pack/pallas_call | solution.py:101
  10.1 0.0 copy-start.2
  10.1 1.3 %copy-done.2 = bf16[32,64,512]{2,1,0:T(8,128)(2,1)} copy-done((bf16[32,64,512]{2,1,0:T(8,128)(2,1)}, bf16[32,64,512]{2,1,0:T(8,128)(2,1)S(1)}, u32[]{:S(2)}) %copy-start.2) | copy-done | bytes 2097176
  11.4 0.0 copy-start.3
  11.4 0.6 copy-done.3
  12.0 102.1 %layer.1 = bf16[8,64,1024]{2,1,0:T(8,128)(2,1)} custom-call(bf16[32,64,512]{2,1,0:T(8,128)(2,1)} %copy-done.2, s32[32,1,128]{2,1,0:T(1,128)} %copy-done.3, f32[1,1024]{1,0:T(1,128)} %gain_ref.1, f32[8,64,128]{2,1,0:T(8,128)} %bitcast.10, bf16[1,1024,1024]{2,1,0:T(8,128)(2,1)} %wq_hbm.1, bf16[1,1024,1024]{2,1,0:T(8,128)(2,1)} %wk_hbm.1, ...), custom_call_target="tpu_custom_call" | custom-call | tf_op jit(solution)/shard_map/layer/pallas_call | solution.py:401
  114.1 2.3 %copy.15 = bf16[512,1024]{1,0:T(8,128)(2,1)} copy(bf16[512,1024]{1,0:T(8,128)(2,1)} %bitcast.9) | data formatting | bytes 2097152
Async XLA Ops:
  0.0 0.7 copy-start
  3.3 2.8 %copy-start.1 = (bf16[48,64,1024]{2,1,0:T(8,128)(2,1)S(1)}, bf16[48,64,1024]{2,1,0:T(8,128)(2,1)}, u32[]{:S(2)}) copy-start(bf16[48,64,1024]{2,1,0:T(8,128)(2,1)} %src_ref.1) | copy-start | bytes 18874372
  6.1 0.7 copy-start.4
  6.8 0.7 copy-start.5
  10.1 1.4 %copy-start.2 = (bf16[32,64,512]{2,1,0:T(8,128)(2,1)}, bf16[32,64,512]{2,1,0:T(8,128)(2,1)S(1)}, u32[]{:S(2)}) copy-start(bf16[32,64,512]{2,1,0:T(8,128)(2,1)S(1)} %get-tuple-element.7.packed_ref) | copy-start | bytes 6291460
  11.4 0.6 copy-start.3

commit v2 on v1

--- a/solution.py
+++ b/solution.py
@@ -139,7 +139,7 @@
 def layer_kernel(
     packed_ref, meta_ref, gain_ref, bias_ref, wq_hbm, wk_hbm, wv_hbm, wo_hbm, out_ref,
     wq, wk, wv, wo, arr, codes, normed, query, key, value, context, part,
-    keep, pair_out, pair_in, mate_out, mate_in, far_out, far_in, mine,
+    scores, probs, totals, keep, pair_out, pair_in, mate_out, mate_in, far_out, far_in, mine,
     wsem, tok_s, tok_r, meta_s, meta_r, fwd_s, fwd_r,
     pair_s, pair_r, mate_s, mate_r, far_s, far_r,
 ):
@@ -255,8 +255,13 @@
         far_out[g] = total.astype(jnp.bfloat16)
         far_copy(g).start()
 
-    row = lax.broadcasted_iota(jnp.int32, (128, 128), 0)
-    col = lax.broadcasted_iota(jnp.int32, (128, 128), 1)
+    row = lax.broadcasted_iota(jnp.int32, (CAP, 128), 0)
+    west = lax.broadcasted_iota(jnp.int32, (CAP, 128), 1) < CAP
+    blank = jnp.zeros((CAP, DK), jnp.bfloat16)
+    ones = (
+        (lax.broadcasted_iota(jnp.int32, (128, 256), 0) < CAP)
+        == (lax.broadcasted_iota(jnp.int32, (128, 256), 1) < DK)
+    ).astype(jnp.bfloat16)
 
     def group(g, _):
         base = g * 4
@@ -292,29 +297,51 @@
                 receive(base + 4 + i)
 
         for block in range(2):
-            code = jnp.where(col[0:1] < CAP, codes[base + 2 * block], codes[base + 2 * block + 1])
-            shift = jnp.where(col[0:1] < CAP, 0, CAP)
-            start = code // 256 + shift
-            end = code % 256 + shift
-            allowed = (row >= start) & (row < end)
-            span = slice(block * 128, block * 128 + 128)
+            code = jnp.where(west[0:1], codes[base + 2 * block], codes[base + 2 * block + 1])
+            allowed = (row >= code // 256) & (row < code % 256)
+            top = slice(block * 128, block * 128 + CAP)
+            low = slice(block * 128 + CAP, block * 128 + 128)
             for h in range(HEADS):
                 lanes = slice(h * DK, h * DK + DK)
+                both = jnp.concatenate([query[top, lanes], query[low, lanes]], axis=1)
+                keys = jnp.concatenate(
+                    [
+                        jnp.concatenate([key[top, lanes], blank], axis=1),
+                        jnp.concatenate([blank, key[low, lanes]], axis=1),
+                    ],
+                    axis=0,
+                )
                 s = lax.dot_general(
-                    query[span, lanes], key[span, lanes], (((1,), (1,)), ((), ())),
-                    preferred_element_type=jnp.float32,
+                    both, keys, (((1,), (1,)), ((), ())), preferred_element_type=jnp.float32
                 )
-                b = bias_ref[h]
-                s = jnp.where(allowed, s + jnp.concatenate([b, b], axis=0), NEG)
-                top = jnp.max(s, axis=-1, keepdims=True)
-                w = jnp.exp(s - top)
-                total = jnp.sum(w, axis=-1, keepdims=True)
-                inverse = jnp.where(top > 0.5 * NEG, 1.0 / total, 0.0)
-                ctx = jnp.dot(
-                    (w * inverse).astype(jnp.bfloat16), value[span, lanes],
-                    preferred_element_type=jnp.float32,
+                scores[block, h] = jnp.where(allowed, s + bias_ref[h], NEG)
+        for block in range(2):
+            for h in range(HEADS):
+                s = scores[block, h]
+                first = jnp.max(jnp.where(west, s, NEG), axis=-1, keepdims=True)
+                second = jnp.max(jnp.where(west, NEG, s), axis=-1, keepdims=True)
+                peak = jnp.maximum(jnp.where(west, first, second), 0.5 * NEG)
+                probs[block, h] = jnp.exp(s - peak).astype(jnp.bfloat16)
+        for block in range(2):
+            top = slice(block * 128, block * 128 + CAP)
+            low = slice(block * 128 + CAP, block * 128 + 128)
+            sums = jnp.dot(
+                probs[block].reshape(HEADS * CAP, 128), ones, preferred_element_type=jnp.float32
+            )
+            totals[block] = (1.0 / jnp.maximum(sums, 0.5)).reshape(HEADS, CAP, 256)
+            for h in range(HEADS):
+                lanes = slice(h * DK, h * DK + DK)
+                values = jnp.concatenate(
+                    [
+                        jnp.concatenate([value[top, lanes], blank], axis=1),
+                        jnp.concatenate([blank, value[low, lanes]], axis=1),
+                    ],
+                    axis=0,
                 )
-                context[span, lanes] = ctx.astype(jnp.bfloat16)
+                ctx = jnp.dot(probs[block, h], values, preferred_element_type=jnp.float32)
+                ctx = (ctx * totals[block, h]).astype(jnp.bfloat16)
+                context[top, lanes] = ctx[:, 0:DK]
+                context[low, lanes] = ctx[:, DK : 2 * DK]
 
         part[...] = jnp.dot(context[...], wo[...], preferred_element_type=jnp.float32)
         far_pair, _, near_plane = planes(g)
@@ -411,6 +438,9 @@
         + [pltpu.VMEM((256, D), bf)] * 5
         + [
             pltpu.VMEM((256, D), f32),
+            pltpu.VMEM((2, HEADS, CAP, 128), f32),
+            pltpu.VMEM((2, HEADS, CAP, 128), bf),
+            pltpu.VMEM((2, HEADS, CAP, 256), f32),
             pltpu.VMEM((2, 128, HALF), f32),
             pltpu.VMEM((GROUPS, 128, HALF), bf),
             pltpu.VMEM((GROUPS, 128, HALF), bf),

time: 117 us -> 84 us (0.72)
  Pallas kernels: 105 us -> 71.7 us
    pallas_call x1, Pallas kernels: 102 us -> 69.1 us  [layer(): pl.pallas_call(layer_kernel, out_shape=jax.ShapeDtypeStruct((8, CAP, D),...]
where the time goes in v2:
time: 84 us; the launch traced here: 83.3 us
  Pallas kernels  71.7 us (85%)
  local copies, waits for them, and re-layouts  9.74 us (12%)
  matrix products  1.88 us (2%)
    pallas_call x1, Pallas kernels, layer(): pl.pallas_call(layer_kernel, out_shape=jax.ShapeDtypeStruct((8, CAP, D),...  69.1 us
    unnamed x13, local copies, waits for them, and re-layouts  8.99 us
    pallas_call x1, Pallas kernels, pack(): pl.pallas_call(pack_kernel, out_shape=(jax.ShapeDtypeStruct((SLOTS, CAP,...  2.63 us
    dot_general x1, matrix products, position_bias(): jnp.einsum('qkb,bh->hqk', match, table, precision=lax.Precision.HIGHEST)  1.88 us

profile of v2, /device:TPU:34, one launch (start us, length us, event | category | flops | bytes accessed | tf_op | source)
XLA Modules:
  0.0 83.3 jit_solution(2730323434826896233)
XLA Ops:
  0.0 0.0 copy-start
  0.0 0.7 copy-done
  0.7 1.9 %fusion = f32[64,128,8]{1,2,0:T(8,128)S(1)} fusion(f32[64,128,32]{1,2,0:T(8,128)} %constant.2.clone, f32[1,32,8]{1,2,0:T(8,128)S(1)} %copy-done), kind=kOutput, calls=%fused_computation.1 | convolution fusion | flops 25165824 | bytes 1311744 | tf_op jit(solution)/shard_map/qkb,bh->hqk/dot_general | solution.py:44
  2.6 0.8 copy.13
  3.3 0.0 copy-start.1
  3.3 2.8 %copy-done.1 = bf16[48,64,1024]{2,1,0:T(8,128)(2,1)S(1)} copy-done((bf16[48,64,1024]{2,1,0:T(8,128)(2,1)S(1)}, bf16[48,64,1024]{2,1,0:T(8,128)(2,1)}, u32[]{:S(2)}) %copy-start.1) | copy-done | bytes 6291480
  6.1 0.0 copy-start.4
  6.1 0.7 copy-done.4
  6.8 0.0 copy-start.5
  6.8 0.7 copy-done.5
  7.4 2.6 %pack.1 = (bf16[32,64,512]{2,1,0:T(8,128)(2,1)S(1)}, s32[32,1,128]{2,1,0:T(1,128)S(1)}) custom-call(s32[48]{0:T(128)S(1)} %copy-done.4, s32[48]{0:T(128)S(1)} %copy-done.5, bf16[48,64,1024]{2,1,0:T(8,128)(2,1)S(1)} %copy-done.1), custom_call_target="tpu_custom_call" | custom-call | tf_op jit(solution)/shard_map/pack/pallas_call | solution.py:101
  10.1 0.0 copy-start.2
  10.1 1.3 %copy-done.2 = bf16[32,64,512]{2,1,0:T(8,128)(2,1)} copy-done((bf16[32,64,512]{2,1,0:T(8,128)(2,1)}, bf16[32,64,512]{2,1,0:T(8,128)(2,1)S(1)}, u32[]{:S(2)}) %copy-start.2) | copy-done | bytes 2097176
  11.4 0.0 copy-start.3
  11.4 0.6 copy-done.3
  12.0 69.1 %layer.1 = bf16[8,64,1024]{2,1,0:T(8,128)(2,1)} custom-call(bf16[32,64,512]{2,1,0:T(8,128)(2,1)} %copy-done.2, s32[32,1,128]{2,1,0:T(1,128)} %copy-done.3, f32[1,1024]{1,0:T(1,128)} %gain_ref.1, f32[8,64,128]{2,1,0:T(8,128)} %bitcast.10, bf16[1,1024,1024]{2,1,0:T(8,128)(2,1)} %wq_hbm.1, bf16[1,1024,1024]{2,1,0:T(8,128)(2,1)} %wk_hbm.1, ...), custom_call_target="tpu_custom_call" | custom-call | tf_op jit(solution)/shard_map/layer/pallas_call | solution.py:428
  81.1 2.3 %copy.15 = bf16[512,1024]{1,0:T(8,128)(2,1)} copy(bf16[512,1024]{1,0:T(8,128)(2,1)} %bitcast.9) | data formatting | bytes 2097152
Async XLA Ops:
  0.0 0.7 copy-start
  3.3 2.8 %copy-start.1 = (bf16[48,64,1024]{2,1,0:T(8,128)(2,1)S(1)}, bf16[48,64,1024]{2,1,0:T(8,128)(2,1)}, u32[]{:S(2)}) copy-start(bf16[48,64,1024]{2,1,0:T(8,128)(2,1)} %src_ref.1) | copy-start | bytes 18874372
  6.1 0.7 copy-start.4
  6.8 0.7 copy-start.5
  10.1 1.4 %copy-start.2 = (bf16[32,64,512]{2,1,0:T(8,128)(2,1)}, bf16[32,64,512]{2,1,0:T(8,128)(2,1)S(1)}, u32[]{:S(2)}) copy-start(bf16[32,64,512]{2,1,0:T(8,128)(2,1)S(1)} %get-tuple-element.7.packed_ref) | copy-start | bytes 6291460
  11.4 0.6 copy-start.3

commit v3 on v2

--- a/solution.py
+++ b/solution.py
@@ -19,102 +19,15 @@
 DK = 128
 NEG = -1e30
 EPS = 1e-6
-
-
-def bucket_grid(extent, buckets):
-    offsets = np.arange(extent)[None, :] - np.arange(extent)[:, None]
-    half_count = buckets // 2
-    upward = np.where(offsets > 0, half_count, 0)
-    distance = np.abs(offsets)
-    exact_limit = half_count // 2
-    ratio = np.maximum(distance, 1) / exact_limit
-    spread_bucket = exact_limit + np.floor(
-        np.log(ratio) / math.log(128.0 / exact_limit) * (half_count - exact_limit)
-    ).astype(np.int32)
-    spread_bucket = np.minimum(spread_bucket, half_count - 1)
-    return (upward + np.where(distance < exact_limit, distance, spread_bucket)).astype(np.int32)
-
-
-def position_bias(table):
-    grid = bucket_grid(CAP, table.shape[0])
-    grid = np.concatenate([grid, grid], axis=1)
-    match = jnp.asarray(
-        (grid[:, :, None] == np.arange(table.shape[0])[None, None, :]).astype(np.float32)
-    )
-    return jnp.einsum("qkb,bh->hqk", match, table, precision=lax.Precision.HIGHEST)
-
-
-def pack_kernel(tenant_ref, length_ref, src_ref, packed_ref, meta_ref, tokens, stage, fill, sems):
-    core = lax.rem(lax.axis_index("tp"), 2)
-    pairs = src_ref.shape[0]
-    step = pairs // 4
-    copies = []
-    for i in range(4):
-        copies.append(
-            pltpu.make_async_copy(
-                src_ref.at[pl.ds(i * step, step), :, pl.ds(pl.multiple_of(core * HALF, HALF), HALF)],
-                tokens.at[pl.ds(i * step, step)],
-                sems.at[i],
-            )
-        )
-        copies[-1].start()
-
-    def clear(u, _):
-        fill[u] = 0
-        return 0
-
-    lax.fori_loop(0, SLOTS, clear, 0)
-    meta_ref[...] = jnp.zeros_like(meta_ref)
-    lane = lax.broadcasted_iota(jnp.int32, (1, 128), 1)
-
-    def place(i, _):
-        u = tenant_ref[i]
-        n = length_ref[i]
-        start = fill[u]
-        fill[u] = start + n
-        code = start * 256 + start + n
-        inside = ((lane % CAP) >= start) & ((lane % CAP) < start + n)
-        meta_ref[u] = jnp.where(inside, code, meta_ref[u])
-        for c in range(4):
-            piece = tokens[i, :, c * 128 : c * 128 + 128].astype(jnp.float32)
-            stage[u, c, pl.ds(start, CAP), :] = piece
-        return 0
-
-    for i in range(4):
-        copies[i].wait()
-        lax.fori_loop(i * step, (i + 1) * step, place, 0)
-    row = lax.broadcasted_iota(jnp.int32, (CAP, 128), 0)
-
-    def finish(u, _):
-        for c in range(4):
-            rows = jnp.where(row < fill[u], stage[u, c, 0:CAP, :], 0.0).astype(jnp.bfloat16)
-            packed_ref[u, :, c * 128 : c * 128 + 128] = rows
-        return 0
-
-    lax.fori_loop(0, SLOTS, finish, 0)
-
-
-def pack(tenant, length, tokens):
-    pairs = tokens.shape[0]
-    smem = pl.BlockSpec(memory_space=pltpu.SMEM)
-    vmem = pl.BlockSpec(memory_space=pltpu.VMEM)
-    return pl.pallas_call(
-        pack_kernel,
-        out_shape=(
-            jax.ShapeDtypeStruct((SLOTS, CAP, HALF), jnp.bfloat16),
-            jax.ShapeDtypeStruct((SLOTS, 1, 128), jnp.int32),
-        ),
-        in_specs=[smem, smem, pl.BlockSpec(memory_space=pl.ANY)],
-        out_specs=(vmem, vmem),
-        scratch_shapes=[
-            pltpu.VMEM((pairs, CAP, HALF), jnp.bfloat16),
-            pltpu.VMEM((SLOTS, 4, 2 * CAP, 128), jnp.float32),
-            pltpu.SMEM((SLOTS,), jnp.int32),
-            pltpu.SemaphoreType.DMA((4,)),
-        ],
-        compiler_params=pltpu.CompilerParams(vmem_limit_bytes=40 * 1024 * 1024),
-        name="pack",
-    )(tenant, length, tokens)
+BUCKETS = 32
+SELF = 16
+
+
+def bucket_limits():
+    distance = np.arange(8, CAP)
+    steps = np.floor(np.log(distance / 8) / math.log(16.0) * 8).astype(np.int32)
+    steps = np.minimum(steps, 7)
+    return [int(distance[steps >= n][0]) for n in range(1, int(steps.max()) + 1)]
 
 
 def here():
@@ -131,26 +44,35 @@
     g = pos // 4
     a = (pos // 2) % 2
     b = pos % 2
-    dz = g % 2 + 2 * a
-    dx = (g // 2 + b) % 4
-    return dz, dx, b
+    odd_z = g % 2
+    odd_x = (g // 2) % 2
+    dl = 1 - g // 4
+    flip = dl * jnp.where(odd_z == odd_x, (a + b) % 2, jnp.where(odd_z == 1, b, a))
+    return odd_z + 2 * a, odd_x + 2 * b, dl, flip
 
 
 def layer_kernel(
-    packed_ref, meta_ref, gain_ref, bias_ref, wq_hbm, wk_hbm, wv_hbm, wo_hbm, out_ref,
-    wq, wk, wv, wo, arr, codes, normed, query, key, value, context, part,
+    tenant_ref, length_ref, table_ref, gain_ref, src_hbm, wq_hbm, wk_hbm, wv_hbm, wo_hbm, out_ref,
+    wq, wk, wv, wo, tokens, pick, packed, spots, meta, bias,
+    arr, codes, normed, query, key, value, context, part,
     scores, probs, totals, keep, pair_out, pair_in, mate_out, mate_in, far_out, far_in, mine,
-    wsem, tok_s, tok_r, meta_s, meta_r, fwd_s, fwd_r,
+    ssem, wsem, tok_s, tok_r, meta_s, meta_r, fwd_s, fwd_r,
     pair_s, pair_r, mate_s, mate_r, far_s, far_r,
 ):
     z, x, lo, hi, core = here()
     tenant = lax.axis_index("tenant")
     partner = device(z, x, lo, hi, core + 1)
+    pairs = src_hbm.shape[0]
+    chunks = pairs * CAP // 128
 
     def peer(pos):
-        dz, dx, dl = shift_of(pos)
-        return device(z + dz, x + dx, lo + dl, hi + dl * ((dz + dx) % 2), core)
-
+        dz, dx, dl, flip = shift_of(pos)
+        return device(z + dz, x + dx, lo + dl, hi + flip, core)
+
+    source = pltpu.make_async_copy(
+        src_hbm.at[:, :, pl.ds(pl.multiple_of(core * HALF, HALF), HALF)], tokens, ssem.at[0]
+    )
+    source.start()
     weights = [
         pltpu.make_async_copy(src.at[0], dst, wsem.at[i])
         for i, (src, dst) in enumerate(((wq_hbm, wq), (wk_hbm, wk), (wv_hbm, wv), (wo_hbm, wo)))
@@ -161,28 +83,75 @@
     barrier = pltpu.get_barrier_semaphore()
 
     def greet(pos, _):
-        pl.semaphore_signal(barrier, inc=1, device_id=peer(pos), device_id_type=MESH)
-        return 0
-
-    lax.fori_loop(1, SLOTS, greet, 0)
+        @pl.when(pos != SELF)
+        def _():
+            pl.semaphore_signal(barrier, inc=1, device_id=peer(pos), device_id_type=MESH)
+
+        return 0
+
+    lax.fori_loop(0, SLOTS, greet, 0)
     pl.semaphore_signal(barrier, inc=1, device_id=partner, device_id_type=MESH)
     for c in range(2):
         pl.semaphore_signal(
             barrier, inc=1, device_id=device(z, x, lo, hi + 1, c), device_id_type=MESH
         )
-    pl.semaphore_wait(barrier, SLOTS + 2)
+
+    lane = lax.broadcasted_iota(jnp.int32, (chunks, 128), 1)
+    pair_of = lax.broadcasted_iota(jnp.int32, (chunks, 128), 0) * 2 + lane // CAP
+    place = lane % CAP
+    slot_of = lax.broadcasted_iota(jnp.int32, (SLOTS, 128), 0)
+    slot_row = lax.broadcasted_iota(jnp.int32, (SLOTS, 128), 1) % CAP
+
+    def spread(j, carry):
+        whose, count = carry
+        here_now = pair_of == j
+        return jnp.where(here_now, tenant_ref[j], whose), jnp.where(here_now, length_ref[j], count)
+
+    nothing = jnp.zeros((chunks, 128), jnp.int32)
+    whose, count = lax.fori_loop(0, pairs, spread, (nothing, nothing))
+
+    def stack(j, carry):
+        offset, fill, code = carry
+        who, size = tenant_ref[j], length_ref[j]
+        offset = offset + jnp.where((whose == who) & (pair_of > j), size, 0)
+        hit = slot_of == who
+        inside = hit & (slot_row >= fill) & (slot_row < fill + size)
+        code = jnp.where(inside, fill * 257 + size, code)
+        return offset, jnp.where(hit, fill + size, fill), code
+
+    empty = jnp.zeros((SLOTS, 128), jnp.int32)
+    offset, _, code = lax.fori_loop(0, pairs, stack, (nothing, empty, empty))
+    spots[...] = jnp.where(place < count, whose * CAP + offset + place, -1)
+    for u in range(SLOTS):
+        meta[u] = code[u : u + 1, :]
+
+    row = lax.broadcasted_iota(jnp.int32, (CAP, 128), 0)
+    west = lax.broadcasted_iota(jnp.int32, (CAP, 128), 1) < CAP
+
+    def pack(g):
+        slots = [peer(g * 4 + s)[0] * CAP for s in range(4)]
+        for m in range(chunks):
+            spot = spots[m : m + 1, :]
+            for s in range(4):
+                pick[s * CAP : s * CAP + CAP, m * 128 : m * 128 + 128] = jnp.where(
+                    row == spot - slots[s], 1.0, 0.0
+                ).astype(jnp.bfloat16)
+        rows = jnp.dot(
+            pick[...], tokens[...].reshape(pairs * CAP, HALF), preferred_element_type=jnp.float32
+        )
+        packed[pl.ds(g * 4, 4)] = rows.astype(jnp.bfloat16).reshape(4, CAP, HALF)
 
     def token_copy(pos):
         target = peer(pos)
         return pltpu.make_async_remote_copy(
-            packed_ref.at[target[0]], arr.at[core, pos], tok_s.at[pos], tok_r.at[pos],
+            packed.at[pos], arr.at[core, pos], tok_s.at[pos], tok_r.at[pos],
             device_id=target, device_id_type=MESH,
         )
 
     def meta_copy(pos):
         target = peer(pos)
         return pltpu.make_async_remote_copy(
-            meta_ref.at[target[0]], codes.at[pos], meta_s.at[pos], meta_r.at[pos],
+            meta.at[target[0]], codes.at[pos], meta_s.at[pos], meta_r.at[pos],
             device_id=target, device_id_type=MESH,
         )
 
@@ -193,32 +162,65 @@
         )
 
     own_forward = pltpu.make_async_remote_copy(
-        packed_ref.at[tenant], arr.at[core, 0], fwd_s.at[0], fwd_r.at[0],
+        packed.at[SELF], arr.at[core, SELF], fwd_s.at[SELF], fwd_r.at[SELF],
         device_id=partner, device_id_type=MESH,
     )
+
     def wait_partner(pos):
         pltpu.make_async_remote_copy(
             arr.at[1 - core, pos], arr.at[1 - core, pos], fwd_s.at[pos], fwd_r.at[pos],
             device_id=partner, device_id_type=MESH,
         ).wait_recv()
 
+    def send(pos):
+        @pl.when(pos != SELF)
+        def _():
+            meta_copy(pos).start()
+            token_copy(pos).start()
+
+    def send_group(g):
+        for i in range(4):
+            send(g * 4 + i)
+
+    source.wait()
+    pack(0)
+    pl.semaphore_wait(barrier, SLOTS + 2)
+
+    def pack_and_send(g, _):
+        pack(g)
+        send_group(g - 1)
+        return 0
+
+    lax.fori_loop(1, GROUPS, pack_and_send, 0)
+    send_group(GROUPS - 1)
     own_forward.start()
-
-    def send(pos, _):
-        meta_copy(pos).start()
-        token_copy(pos).start()
-        return 0
-
-    lax.fori_loop(1, SLOTS, send, 0)
-    arr[core, 0] = packed_ref[tenant]
-    codes[0] = meta_ref[tenant]
+    arr[core, SELF] = packed[SELF]
+    codes[SELF] = meta[tenant]
+
+    ahead = lax.broadcasted_iota(jnp.int32, (CAP, 128), 1) % CAP - row
+    distance = jnp.abs(ahead)
+    bucket = jnp.where(distance < 8, distance, 8)
+    for limit in bucket_limits():
+        bucket = bucket + jnp.where(distance >= limit, 1, 0)
+    bucket = bucket + jnp.where(ahead > 0, 16, 0)
+
+    def expand(h, _):
+        total = jnp.zeros((CAP, 128), jnp.float32)
+        for k in range(BUCKETS):
+            total = jnp.where(bucket == k, table_ref[h, k], total)
+        bias[h] = total
+        return 0
+
+    lax.fori_loop(0, HEADS, expand, 0)
 
     def receive(pos):
-        token_copy(pos).wait_recv()
-        meta_copy(pos).wait_recv()
-        forward_copy(pos).start()
-
-    for pos in range(1, 4):
+        @pl.when(pos != SELF)
+        def _():
+            token_copy(pos).wait_recv()
+            meta_copy(pos).wait_recv()
+            forward_copy(pos).start()
+
+    for pos in range(4):
         receive(pos)
 
     def planes(g):
@@ -255,8 +257,6 @@
         far_out[g] = total.astype(jnp.bfloat16)
         far_copy(g).start()
 
-    row = lax.broadcasted_iota(jnp.int32, (CAP, 128), 0)
-    west = lax.broadcasted_iota(jnp.int32, (CAP, 128), 1) < CAP
     blank = jnp.zeros((CAP, DK), jnp.bfloat16)
     ones = (
         (lax.broadcasted_iota(jnp.int32, (128, 256), 0) < CAP)
@@ -314,7 +314,7 @@
                 s = lax.dot_general(
                     both, keys, (((1,), (1,)), ((), ())), preferred_element_type=jnp.float32
                 )
-                scores[block, h] = jnp.where(allowed, s + bias_ref[h], NEG)
+                scores[block, h] = jnp.where(allowed, s + bias[h], NEG)
         for block in range(2):
             for h in range(HEADS):
                 s = scores[block, h]
@@ -382,7 +382,8 @@
             ).wait_recv()
         for b in range(2):
             pos = g * 4 + near_pair * 2 + b
-            src_slot = ((x + 8 - q - b) % 4) * 2 + (lo + b) % 2
+            _, dx, dl, _ = shift_of(pos)
+            src_slot = ((x + 4 - dx) % 4) * 2 + (lo + dl) % 2
             span = slice(b * CAP, b * CAP + CAP)
             for c in range(2):
                 cols = slice(c * HALF, c * HALF + HALF)
@@ -398,13 +399,16 @@
     lax.fori_loop(0, 4, combine, 0)
 
     def drain(pos, _):
-        token_copy(pos).wait_send()
-        meta_copy(pos).wait_send()
-        forward_copy(pos).wait_send()
+        @pl.when(pos != SELF)
+        def _():
+            token_copy(pos).wait_send()
+            meta_copy(pos).wait_send()
+            forward_copy(pos).wait_send()
+
         return 0
 
     own_forward.wait_send()
-    lax.fori_loop(1, SLOTS, drain, 0)
+    lax.fori_loop(0, SLOTS, drain, 0)
 
     def drain_groups(g, _):
         pair_copy(g).wait_send()
@@ -420,7 +424,9 @@
     lax.fori_loop(0, 4, drain_mates, 0)
 
 
-def layer(packed, meta, gain, bias, wq, wk, wv, wo):
+def layer(tenant, length, table, gain, tokens, wq, wk, wv, wo):
+    pairs = tokens.shape[0]
+    smem = pl.BlockSpec(memory_space=pltpu.SMEM)
     vmem = pl.BlockSpec(memory_space=pltpu.VMEM)
     anywhere = pl.BlockSpec(memory_space=pl.ANY)
     bf, f32 = jnp.bfloat16, jnp.float32
@@ -428,10 +434,16 @@
     return pl.pallas_call(
         layer_kernel,
         out_shape=jax.ShapeDtypeStruct((8, CAP, D), bf),
-        in_specs=[vmem] * 4 + [anywhere] * 4,
+        in_specs=[smem] * 3 + [vmem] + [anywhere] * 5,
         out_specs=vmem,
         scratch_shapes=[pltpu.VMEM((D, D), bf)] * 4
         + [
+            pltpu.VMEM((pairs, CAP, HALF), bf),
+            pltpu.VMEM((256, pairs * CAP), bf),
+            pltpu.VMEM((SLOTS, CAP, HALF), bf),
+            pltpu.VMEM((pairs * CAP // 128, 128), jnp.int32),
+            pltpu.VMEM((SLOTS, 1, 128), jnp.int32),
+            pltpu.VMEM((HEADS, CAP, 128), f32),
             pltpu.VMEM((2, SLOTS, CAP, HALF), bf),
             pltpu.VMEM((SLOTS, 1, 128), jnp.int32),
         ]
@@ -449,23 +461,24 @@
             pltpu.VMEM((GROUPS, 128, HALF), bf),
             pltpu.VMEM((2, 4, 128, HALF), bf),
             pltpu.VMEM((4, 128, D), f32),
-            dma((4,)), dma((SLOTS,)), dma((SLOTS,)), dma((SLOTS,)), dma((SLOTS,)),
+            dma((1,)), dma((4,)), dma((SLOTS,)), dma((SLOTS,)), dma((SLOTS,)), dma((SLOTS,)),
             dma((SLOTS,)), dma((SLOTS,)),
             dma((GROUPS,)), dma((GROUPS,)), dma((4,)), dma((4,)), dma((GROUPS,)), dma((2, 4)),
         ],
         compiler_params=pltpu.CompilerParams(
-            collective_id=0, has_side_effects=True, vmem_limit_bytes=56 * 1024 * 1024
+            collective_id=0, has_side_effects=True, vmem_limit_bytes=67_043_328
         ),
         name="layer",
-    )(packed, meta, gain, bias, wq, wk, wv, wo)
+    )(tenant, length, table, gain, tokens, wq, wk, wv, wo)
 
 
 def per_device(
     src_tokens, pair_tenant, pair_length, norm_gain, w_query, w_key, w_value, w_out, rel_bias
 ):
-    packed, meta = pack(pair_tenant, pair_length, src_tokens)
-    bias = position_bias(rel_bias[0])
-    out = layer(packed, meta, norm_gain, bias, w_query, w_key, w_value, w_out)
+    table = jnp.transpose(rel_bias[0])
+    out = layer(
+        pair_tenant, pair_length, table, norm_gain, src_tokens, w_query, w_key, w_value, w_out
+    )
     return out.reshape(8 * CAP, D)
 
 

time: 84 us -> 63.5 us (0.76)
  Pallas kernels: 71.7 us -> 61.1 us
  local copies, waits for them, and re-layouts: 9.74 us -> 2.26 us
  matrix products: 1.88 us -> 0 us
    pallas_call x1, Pallas kernels: 69.1 us -> 61.1 us  [layer(): pl.pallas_call(layer_kernel, out_shape=jax.ShapeDtypeStruct((8, CAP, D),...]
    unnamed x13 -> x1, local copies, waits for them, and re-layouts: 8.99 us -> 2.26 us
    pallas_call x1 -> x0, Pallas kernels: 2.63 us -> none  [pack(): pl.pallas_call(pack_kernel, out_shape=(jax.ShapeDtypeStruct((SLOTS, CAP,...]
    dot_general x1 -> x0, matrix products: 1.88 us -> none  [position_bias(): jnp.einsum('qkb,bh->hqk', match, table, precision=lax.Precision.HIGHEST)]
where the time goes in v3:
time: 63.5 us; the launch traced here: 63.3 us
  Pallas kernels  61.1 us (96%)
  local copies, waits for them, and re-layouts  2.26 us (4%)
    pallas_call x1, Pallas kernels, layer(): pl.pallas_call(layer_kernel, out_shape=jax.ShapeDtypeStruct((8, CAP, D),...  61.1 us
    unnamed x1, local copies, waits for them, and re-layouts  2.26 us

profile of v3, /device:TPU:34, one launch (start us, length us, event | category | flops | bytes accessed | tf_op | source)
XLA Modules:
  0.0 63.3 jit_solution(9028430233337409604)
XLA Ops:
  0.0 61.1 %layer.1 = bf16[8,64,1024]{2,1,0:T(8,128)(2,1)} custom-call(s32[48]{0:T(128)} %tenant_ref.1, s32[48]{0:T(128)} %length_ref.1, f32[8,32]{1,0:T(8,128)} %bitcast.5, f32[1,1024]{1,0:T(1,128)} %gain_ref.1, bf16[48,64,1024]{2,1,0:T(8,128)(2,1)} %src_hbm.1, bf16[1,1024,1024]{2,1,0:T(8,128)(2,1)} %wq_hbm.1, bf16[1,1024,1024]{2,1,0:T(8,128)(2,1)} %wk_hbm.1, ...), custom_call_target="tpu_custom_call" | custom-call | tf_op jit(solution)/shard_map/layer/pallas_call | solution.py:434
  61.1 2.3 %copy.11 = bf16[512,1024]{1,0:T(8,128)(2,1)} copy(bf16[512,1024]{1,0:T(8,128)(2,1)} %bitcast.4) | data formatting | bytes 2097152

commit v4 on v3

--- a/solution.py
+++ b/solution.py
@@ -30,24 +30,42 @@
     return [int(distance[steps >= n][0]) for n in range(1, int(steps.max()) + 1)]
 
 
+def unrolled(count, body, carry):
+    def steps(block, carry):
+        for i in range(12):
+            carry = body(block * 12 + i, carry)
+        return carry
+
+    return lax.fori_loop(0, count // 12, steps, carry)
+
+
+def mod(a, b):
+    return a % b if isinstance(a, int) else lax.rem(a, jnp.int32(b))
+
+
+def div(a, b):
+    return a // b if isinstance(a, int) else lax.div(a, jnp.int32(b))
+
+
 def here():
     t = lax.axis_index("tenant")
     p = lax.axis_index("tp")
-    return t // 8, (t // 2) % 4, t % 2, p // 2, p % 2
+    return div(t, 8), mod(div(t, 2), 4), mod(t, 2), div(p, 2), mod(p, 2)
 
 
 def device(z, x, lo, hi, core):
-    return ((z % 4) * 8 + (x % 4) * 2 + lo % 2, (hi % 2) * 2 + core % 2)
+    return (mod(z, 4) * 8 + mod(x, 4) * 2 + mod(lo, 2), mod(hi, 2) * 2 + mod(core, 2))
 
 
 def shift_of(pos):
-    g = pos // 4
-    a = (pos // 2) % 2
-    b = pos % 2
-    odd_z = g % 2
-    odd_x = (g // 2) % 2
-    dl = 1 - g // 4
-    flip = dl * jnp.where(odd_z == odd_x, (a + b) % 2, jnp.where(odd_z == 1, b, a))
+    g = div(pos, 4)
+    a = mod(div(pos, 2), 2)
+    b = mod(pos, 2)
+    odd_z = mod(g, 2)
+    odd_x = mod(div(g, 2), 2)
+    dl = 1 - div(g, 4)
+    same = 1 - mod(odd_z + odd_x, 2)
+    flip = dl * mod((same + (1 - same) * (1 - odd_z)) * a + (same + (1 - same) * odd_z) * b, 2)
     return odd_z + 2 * a, odd_x + 2 * b, dl, flip
 
 
@@ -82,14 +100,9 @@
 
     barrier = pltpu.get_barrier_semaphore()
 
-    def greet(pos, _):
-        @pl.when(pos != SELF)
-        def _():
+    for pos in range(SLOTS):
+        if pos != SELF:
             pl.semaphore_signal(barrier, inc=1, device_id=peer(pos), device_id_type=MESH)
-
-        return 0
-
-    lax.fori_loop(0, SLOTS, greet, 0)
     pl.semaphore_signal(barrier, inc=1, device_id=partner, device_id_type=MESH)
     for c in range(2):
         pl.semaphore_signal(
@@ -108,7 +121,7 @@
         return jnp.where(here_now, tenant_ref[j], whose), jnp.where(here_now, length_ref[j], count)
 
     nothing = jnp.zeros((chunks, 128), jnp.int32)
-    whose, count = lax.fori_loop(0, pairs, spread, (nothing, nothing))
+    whose, count = unrolled(pairs, spread, (nothing, nothing))
 
     def stack(j, carry):
         offset, fill, code = carry
@@ -120,7 +133,7 @@
         return offset, jnp.where(hit, fill + size, fill), code
 
     empty = jnp.zeros((SLOTS, 128), jnp.int32)
-    offset, _, code = lax.fori_loop(0, pairs, stack, (nothing, empty, empty))
+    offset, _, code = unrolled(pairs, stack, (nothing, empty, empty))
     spots[...] = jnp.where(place < count, whose * CAP + offset + place, -1)
     for u in range(SLOTS):
         meta[u] = code[u : u + 1, :]
@@ -187,8 +200,8 @@
     pl.semaphore_wait(barrier, SLOTS + 2)
 
     def pack_and_send(g, _):
+        send_group(g - 1)
         pack(g)
-        send_group(g - 1)
         return 0
 
     lax.fori_loop(1, GROUPS, pack_and_send, 0)

time: 63.5 us -> 62.2 us (0.980)
  Pallas kernels: 61.1 us -> 59.5 us
    pallas_call x1, Pallas kernels: 61.1 us -> 59.5 us  [layer(): pl.pallas_call(layer_kernel, out_shape=jax.ShapeDtypeStruct((8, CAP, D),...]
where the time goes in v4:
time: 62.2 us; the launch traced here: 61.7 us
  Pallas kernels  59.5 us (96%)
  local copies, waits for them, and re-layouts  2.26 us (4%)
    pallas_call x1, Pallas kernels, layer(): pl.pallas_call(layer_kernel, out_shape=jax.ShapeDtypeStruct((8, CAP, D),...  59.5 us
    unnamed x1, local copies, waits for them, and re-layouts  2.26 us

profile of v4, /device:TPU:34, one launch (start us, length us, event | category | flops | bytes accessed | tf_op | source)
XLA Modules:
  0.0 61.7 jit_solution(6892790163734525798)
XLA Ops:
  0.0 59.5 %layer.1 = bf16[8,64,1024]{2,1,0:T(8,128)(2,1)} custom-call(s32[48]{0:T(128)} %tenant_ref.1, s32[48]{0:T(128)} %length_ref.1, f32[8,32]{1,0:T(8,128)} %bitcast.5, f32[1,1024]{1,0:T(1,128)} %gain_ref.1, bf16[48,64,1024]{2,1,0:T(8,128)(2,1)} %src_hbm.1, bf16[1,1024,1024]{2,1,0:T(8,128)(2,1)} %wq_hbm.1, bf16[1,1024,1024]{2,1,0:T(8,128)(2,1)} %wk_hbm.1, ...), custom_call_target="tpu_custom_call" | custom-call | tf_op jit(solution)/shard_map/layer/pallas_call | solution.py:447
  59.5 2.3 %copy.11 = bf16[512,1024]{1,0:T(8,128)(2,1)} copy(bf16[512,1024]{1,0:T(8,128)(2,1)} %bitcast.4) | data formatting | bytes 2097152

commit v5 on v4

--- a/solution.py
+++ b/solution.py
@@ -210,6 +210,16 @@
     arr[core, SELF] = packed[SELF]
     codes[SELF] = meta[tenant]
 
+    def receive(pos):
+        @pl.when(pos != SELF)
+        def _():
+            token_copy(pos).wait_recv()
+            meta_copy(pos).wait_recv()
+            forward_copy(pos).start()
+
+    for pos in range(4):
+        receive(pos)
+
     ahead = lax.broadcasted_iota(jnp.int32, (CAP, 128), 1) % CAP - row
     distance = jnp.abs(ahead)
     bucket = jnp.where(distance < 8, distance, 8)
@@ -225,16 +235,6 @@
         return 0
 
     lax.fori_loop(0, HEADS, expand, 0)
-
-    def receive(pos):
-        @pl.when(pos != SELF)
-        def _():
-            token_copy(pos).wait_recv()
-            meta_copy(pos).wait_recv()
-            forward_copy(pos).start()
-
-    for pos in range(4):
-        receive(pos)
 
     def planes(g):
         first = (z + 4 - g % 2) % 4

time: 62.2 us -> 62.2 us (level)
  no operation moved by 1% of the time
where the time goes in v5:
time: 62.2 us; the launch traced here: 61.7 us
  Pallas kernels  59.5 us (96%)
  local copies, waits for them, and re-layouts  2.26 us (4%)
    pallas_call x1, Pallas kernels, layer(): pl.pallas_call(layer_kernel, out_shape=jax.ShapeDtypeStruct((8, CAP, D),...  59.5 us
    unnamed x1, local copies, waits for them, and re-layouts  2.26 us

profile of v5, /device:TPU:34, one launch (start us, length us, event | category | flops | bytes accessed | tf_op | source)
XLA Modules:
  0.0 61.7 jit_solution(12286365010617949067)
XLA Ops:
  0.0 59.5 %layer.1 = bf16[8,64,1024]{2,1,0:T(8,128)(2,1)} custom-call(s32[48]{0:T(128)} %tenant_ref.1, s32[48]{0:T(128)} %length_ref.1, f32[8,32]{1,0:T(8,128)} %bitcast.5, f32[1,1024]{1,0:T(1,128)} %gain_ref.1, bf16[48,64,1024]{2,1,0:T(8,128)(2,1)} %src_hbm.1, bf16[1,1024,1024]{2,1,0:T(8,128)(2,1)} %wq_hbm.1, bf16[1,1024,1024]{2,1,0:T(8,128)(2,1)} %wk_hbm.1, ...), custom_call_target="tpu_custom_call" | custom-call | tf_op jit(solution)/shard_map/layer/pallas_call | solution.py:447
  59.5 2.3 %copy.11 = bf16[512,1024]{1,0:T(8,128)(2,1)} copy(bf16[512,1024]{1,0:T(8,128)(2,1)} %bitcast.4) | data formatting | bytes 2097152
